TPU v7x, 256 devices: a whole 4x4x8 slice. The times are simulated.
256 devices in a mesh: row: 8 (over y, core), col: 4 (over x), layer: 8 (over z).
Axes of the slice: x: 4, y: 4, z: 8, core: 2. Of those that a mesh axis runs over, the one named last changes fastest.
Arguments:
- hamiltonian: bfloat16 [5120, 5120], P(('row', 'layer'), 'col'), may hold values from -1.2 to 1.2, as said below
- tile_pattern: int32 [40, 40], replicated, may hold values from 0 to 1, as said below
- n_occ: int32 [1], replicated, may hold values from 1024 to 4095
- mu: float32 [1], replicated, may hold values from -0.2 to 0.2
- gamma: float32 [1], replicated, may hold values from 0.25 to 0.4
Outputs:
- density: float32 [5120, 5120], P(('row', 'layer'), 'col')
Inputs may be any that keep to these rules, and one draw needn't show every extreme that they name: `tile_pattern`: Symmetric, 0 or 1, with ones on the diagonal and next to it. `hamiltonian`: Symmetric; its eigenvalues lie within -1.8 and 1.8.
All inputs are finite; a program needn't handle non-finite values.
Results may differ from a plain program's by a relative error of at most 0.0055.
Values may be sent and summed in bfloat16 or wider, within the bound.
No kernel may reach another device: no remote copies, remote signals or barrier semaphores. Data moves between devices by JAX's collectives and lax.ppermute only.
A program may use at most 64 MiB of HBM per device.

v0:
```python
import jax
import jax.numpy as jnp
from jax import lax
from jax.sharding import PartitionSpec as P

TILE = 128
STEPS = 2


def element_mask(tile_pattern, row_start, row_count, col_start, col_count):
    tile_count = tile_pattern.shape[0]
    tile_ids = jnp.arange(tile_count, dtype=jnp.int32)
    row_tiles = (row_start + jnp.arange(row_count, dtype=jnp.int32)) // TILE
    col_tiles = (col_start + jnp.arange(col_count, dtype=jnp.int32)) // TILE
    row_hot = (row_tiles[:, None] == tile_ids[None, :]).astype(jnp.bfloat16)
    col_hot = (tile_ids[:, None] == col_tiles[None, :]).astype(jnp.bfloat16)
    picked = jnp.dot(row_hot, tile_pattern.astype(jnp.bfloat16), preferred_element_type=jnp.float32)
    return jnp.dot(picked.astype(jnp.bfloat16), col_hot, preferred_element_type=jnp.float32)


def shards(hamiltonian, tile_pattern, n_occ, mu, gamma):
    share_rows, band_cols = hamiltonian.shape
    n_col = lax.axis_size("col")
    n_layer = lax.axis_size("layer")
    order = band_cols * n_col
    layer_index = lax.axis_index("layer")
    row_start = (lax.axis_index("row") * n_layer + layer_index) * share_rows
    col_start = lax.axis_index("col") * band_cols
    mask = element_mask(tile_pattern, row_start, share_rows, col_start, band_cols)
    row_global = row_start + jnp.arange(share_rows, dtype=jnp.int32)
    col_global = col_start + jnp.arange(band_cols, dtype=jnp.int32)
    identity = (row_global[:, None] == col_global[None, :]).astype(jnp.float32)
    filling = n_occ[0].astype(jnp.float32) / order
    start = mask * (
        filling * identity + gamma[0] * (mu[0] * identity - hamiltonian.astype(jnp.float32))
    )
    current = start.astype(jnp.bfloat16)
    result = start
    for iteration in range(STEPS):
        column = lax.all_gather(current, ("row", "layer"), axis=0, tiled=True)

        def rows_product(left_share):
            return jnp.dot(
                lax.all_gather(left_share, "col", axis=1, tiled=True),
                column,
                preferred_element_type=jnp.float32,
            )

        square = mask * rows_product(current)
        cube = mask * rows_product(square.astype(jnp.bfloat16))
        result = 3.0 * square - 2.0 * cube
        current = result.astype(jnp.bfloat16)
    return result


def solution(mesh):
    placed = (P(("row", "layer"), "col"), P(), P(), P(), P())
    return jax.shard_map(
        shards, mesh=mesh, in_specs=placed, out_specs=P(("row", "layer"), "col"), check_vma=False
    )
```

profile of v0, /device:TPU:2, one launch (start us, length us, event | category | flops | bytes accessed | tf_op | source)
XLA Modules:
  0.0 248.6 jit_solution(11599922052640103232)
XLA Ops:
  6.5 0.0 all-gather.3.cloned.1.call-start
  8.5 2.0 fusion.8
  10.5 0.0 all-gather.3.cloned.1.call-update
  10.6 0.0 all-gather.5.cloned.1.call-start
  10.6 14.4 %all_gather.18 = bf16[80,5120]{1,0:T(8,128)(2,1)S(1)} all-gather(bf16[80,1280]{1,0:T(8,128)(2,1)} %get-tuple-element.5), channel_id=1, replica_groups=mesh['row'=8,'col'=4,'layer'=8] {'col'}, dimensions={1}, use_global_device_ids=true | all-gather | bytes 1024000 | tf_op jit(solution)/shard_map/all_gather | solution.py:44
  25.0 79.3 %all-gather.3.cloned.1.call-done = bf16[5120,1280]{1,0:T(8,128)(2,1)} async-done(((bf16[80,1280]{1,0:T(8,128)(2,1)}), bf16[5120,1280]{1,0:T(8,128)(2,1)}) %all-gather.3.cloned.1.call-update) | async-done | bytes 13107216 | tf_op jit(solution)/shard_map/all_gather | solution.py:40
  104.3 0.0 copy-start
  104.3 7.2 %fusion.21 = (bf16[80,1280]{1,0:T(8,128)(2,1)S(1)}, f32[80,1280]{1,0:T(8,128)S(1)}) fusion(f32[80,1280]{1,0:T(8,128)S(1)} %get-tuple-element.6, bf16[80,5120]{1,0:T(8,128)(2,1)S(1)} %all_gather.18, bf16[5120,1280]{1,0:T(8,128)(2,1)} %all-gather.3.cloned.1.call-done), kind=kOutput, calls=%fused_computation.37 | convolution fusion | flops 1048780800 | bytes 14950400 | tf_op jit(solution)/shard_map/dot_general | solution.py:43
  111.6 14.6 %all_gather.20 = bf16[80,5120]{1,0:T(8,128)(2,1)S(1)} all-gather(bf16[80,1280]{1,0:T(8,128)(2,1)S(1)} %get-tuple-element.7), channel_id=1, replica_groups=mesh['row'=8,'col'=4,'layer'=8] {'col'}, dimensions={1}, use_global_device_ids=true | all-gather | bytes 1024000 | tf_op jit(solution)/shard_map/all_gather | solution.py:44
  126.2 0.0 copy-done
  126.2 3.1 %fusion.4 = bf16[80,1280]{1,0:T(8,128)(2,1)} fusion(f32[80,1280]{1,0:T(8,128)S(1)} %get-tuple-element.6, bf16[80,5120]{1,0:T(8,128)(2,1)S(1)} %all_gather.20, bf16[5120,1280]{1,0:T(8,128)(2,1)S(1)} %copy-done, f32[80,1280]{1,0:T(8,128)S(1)} %get-tuple-element.8), kind=kOutput, calls=%fused_computation.8 | convolution fusion | flops 1049088000 | bytes 14950400 | tf_op jit(solution)/shard_map/dot_general | solution.py:43
  129.2 0.0 all-gather.5.cloned.1.call-update
  129.3 13.6 %all_gather.21 = bf16[80,5120]{1,0:T(8,128)(2,1)S(1)} all-gather(bf16[80,1280]{1,0:T(8,128)(2,1)} %fusion.4), channel_id=1, replica_groups=mesh['row'=8,'col'=4,'layer'=8] {'col'}, dimensions={1}, use_global_device_ids=true | all-gather | bytes 1024000 | tf_op jit(solution)/shard_map/all_gather | solution.py:44
  142.8 73.9 %all-gather.5.cloned.1.call-done = bf16[5120,1280]{1,0:T(8,128)(2,1)} async-done(((bf16[80,1280]{1,0:T(8,128)(2,1)}), bf16[5120,1280]{1,0:T(8,128)(2,1)}) %all-gather.5.cloned.1.call-update) | async-done | bytes 13107216 | tf_op jit(solution)/shard_map/all_gather | solution.py:40
  216.7 0.0 copy-start.1
  216.8 7.2 %fusion.22 = (bf16[80,1280]{1,0:T(8,128)(2,1)S(1)}, f32[80,1280]{1,0:T(8,128)S(1)}) fusion(f32[80,1280]{1,0:T(8,128)S(1)} %get-tuple-element.6, bf16[80,5120]{1,0:T(8,128)(2,1)S(1)} %all_gather.21, bf16[5120,1280]{1,0:T(8,128)(2,1)} %all-gather.5.cloned.1.call-done), kind=kOutput, calls=%fused_computation.38 | convolution fusion | flops 1048780800 | bytes 14950400 | tf_op jit(solution)/shard_map/dot_general | solution.py:43
  224.0 14.6 %all_gather.23 = bf16[80,5120]{1,0:T(8,128)(2,1)S(1)} all-gather(bf16[80,1280]{1,0:T(8,128)(2,1)S(1)} %get-tuple-element.9), channel_id=1, replica_groups=mesh['row'=8,'col'=4,'layer'=8] {'col'}, dimensions={1}, use_global_device_ids=true | all-gather | bytes 1024000 | tf_op jit(solution)/shard_map/all_gather | solution.py:44
  238.6 0.0 copy-done.1
  238.6 3.1 %fusion.2 = f32[80,1280]{1,0:T(8,128)} fusion(f32[80,1280]{1,0:T(8,128)S(1)} %get-tuple-element.6, bf16[80,5120]{1,0:T(8,128)(2,1)S(1)} %all_gather.23, bf16[5120,1280]{1,0:T(8,128)(2,1)S(1)} %copy-done.1, f32[80,1280]{1,0:T(8,128)S(1)} %get-tuple-element.10), kind=kOutput, calls=%fused_computation.6 | convolution fusion | flops 1048985600 | bytes 15155200 | tf_op jit(solution)/shard_map/dot_general | solution.py:43
  (2 shorter events, 0.0 us)
Async XLA Ops:
  6.5 97.8 %all-gather.3.cloned.1.call-start = ((), (), s32[]{:S(2)}) async-start(), calls=%async_computation | async-start | bytes 13312000 | tf_op jit(solution)/shard_map/all_gather | solution.py:40
  10.6 206.2 %all-gather.5.cloned.1.call-start = ((), (), s32[]{:S(2)}) async-start(), calls=%async_computation.1 | async-start | bytes 13312000 | tf_op jit(solution)/shard_map/all_gather | solution.py:40
  104.3 21.9 %copy-start = (bf16[5120,1280]{1,0:T(8,128)(2,1)S(1)}, bf16[5120,1280]{1,0:T(8,128)(2,1)}, u32[]{:S(2)}) copy-start(bf16[5120,1280]{1,0:T(8,128)(2,1)} %all-gather.3.cloned.1.call-done) | copy-start | bytes 39321604
  216.7 21.8 %copy-start.1 = (bf16[5120,1280]{1,0:T(8,128)(2,1)S(1)}, bf16[5120,1280]{1,0:T(8,128)(2,1)}, u32[]{:S(2)}) copy-start(bf16[5120,1280]{1,0:T(8,128)(2,1)} %all-gather.5.cloned.1.call-done) | copy-start | bytes 39321604
Sparse Core Ops, SparseCore 0:
  10.7 93.5 all-gather.2
  129.4 87.3 all-gather.4
where the time goes:
time: 249 us
  waiting for transfers between devices  153 us (61%)
  blocking collectives  57.2 us (23%)
  matrix products  22.7 us (9%)
  between operations  15.4 us (6%)
    all_gather x2, waiting for transfers between devices, shards(): column = lax.all_gather(current, ('row', 'layer'), axis=0, tiled=True)  153 us
    all_gather x4, blocking collectives, rows_product(): lax.all_gather(left_share, 'col', axis=1, tiled=True)  57.2 us
    dot_general x4, matrix products, rows_product(): jnp.dot(lax.all_gather(left_share, 'col', axis=1, tiled=True), column, pr...  20.7 us
  transfers between devices with their start and end apart: 2, of which 2 were waited for; matrix products, arithmetic and copies ran while one was open for 0% of the time, Pallas kernels for 0%

commit v1 on v0

--- a/solution.py
+++ b/solution.py
@@ -5,6 +5,28 @@
 
 TILE = 128
 STEPS = 2
+
+
+def in_order(tiles, dim):
+    dims = list(tiles.shape[1:])
+    dims[dim] *= tiles.shape[0]
+    return jnp.moveaxis(tiles, 0, dim).reshape(dims)
+
+
+def ring_gather(value, axis, dim):
+    count = lax.axis_size(axis)
+    pairs = [(i, (i + 1) % count) for i in range(count)]
+    back = [(b, a) for a, b in pairs]
+    lower, upper = ([], [])
+    for step in range(count - 1):
+        if step % 2 == 0:
+            lower.append(lax.ppermute(lower[-1] if lower else value, axis, pairs))
+        else:
+            upper.append(lax.ppermute(upper[-1] if upper else value, axis, back))
+    blocks = jnp.stack([*lower[::-1], value, *upper])
+    shift = lax.axis_index(axis) - len(lower)
+    blocks = blocks[(jnp.arange(count) - shift) % count]
+    return in_order(blocks, dim)
 
 
 def element_mask(tile_pattern, row_start, row_count, col_start, col_count):
@@ -41,9 +63,7 @@
 
         def rows_product(left_share):
             return jnp.dot(
-                lax.all_gather(left_share, "col", axis=1, tiled=True),
-                column,
-                preferred_element_type=jnp.float32,
+                ring_gather(left_share, "col", 1), column, preferred_element_type=jnp.float32
             )
 
         square = mask * rows_product(current)

time: 249 us -> 260 us (1.044)
  blocking collectives: 57.2 us -> 0 us
  waiting for transfers between devices: 153 us -> 191 us
  starting transfers between devices: 0.04 us -> 14.7 us
  matrix products: 22.7 us -> 31.9 us
  local copies, waits for them, and re-layouts: 0.01 us -> 2.64 us
    all_gather x4 -> x0, blocking collectives: 57.2 us -> none  [rows_product(): lax.all_gather(left_share, 'col', axis=1, tiled=True)]
    ppermute x0 -> x12, waiting for transfers between devices: none -> 39.9 us  [the longest x8 39.9 us: ring_gather(): lower.append(lax.ppermute(lower[-1] if lower else value, axis, pairs))]
    ppermute x0 -> x12, starting transfers between devices: none -> 14.6 us  [the longest x8 11.1 us: ring_gather(): lower.append(lax.ppermute(lower[-1] if lower else value, axis, pairs))]
    dot_general x4, matrix products: 20.7 us -> 29.8 us  [rows_product(): jnp.dot(ring_gather(left_share, 'col', 1), column, preferred_element_type...]
  transfers between devices with their start and end apart: 2 -> 14, of which waited for: 2 -> 10; matrix products, arithmetic and copies ran while one was open for 0% -> 1% of each run, Pallas kernels for 0% -> 0%
where the time goes in v1:
time: 260 us; the launch traced here: 258 us
  waiting for transfers between devices  191 us (73%)
  matrix products  31.9 us (12%)
  between operations  15.5 us (6%)
  starting transfers between devices  14.7 us (6%)
  local copies, waits for them, and re-layouts  2.64 us (1%)
    all_gather x2, waiting for transfers between devices, shards(): column = lax.all_gather(current, ('row', 'layer'), axis=0, tiled=True)  151 us
    ppermute x8, waiting for transfers between devices, ring_gather(): lower.append(lax.ppermute(lower[-1] if lower else value, axis, pairs))  39.9 us
    dot_general x4, matrix products, rows_product(): jnp.dot(ring_gather(left_share, 'col', 1), column, preferred_element_type...  29.8 us
    ppermute x8, starting transfers between devices, ring_gather(): lower.append(lax.ppermute(lower[-1] if lower else value, axis, pairs))  11.1 us
  transfers between devices with their start and end apart: 14, of which 10 were waited for; matrix products, arithmetic and copies ran while one was open for 1% of the time, Pallas kernels for 0%

profile of v1, /device:TPU:2, one launch (start us, length us, event | category | flops | bytes accessed | tf_op | source)
XLA Modules:
  0.0 257.8 jit_solution(14285584119065555538)
XLA Ops:
  6.5 0.0 all-gather.3.cloned.1.call-start
  8.5 2.0 fusion.8
  10.5 0.0 all-gather.3.cloned.1.call-update
  10.6 0.0 all-gather.5.cloned.1.call-start
  10.6 1.6 collective-permute-start
  12.2 0.8 collective-permute-start.2
  13.0 4.7 %collective-permute-done = bf16[80,1280]{1,0:T(8,128)(2,1)S(1)} collective-permute-done((bf16[80,1280]{1,0:T(8,128)(2,1)}, bf16[80,1280]{1,0:T(8,128)(2,1)S(1)}, u32[]{:S(2)}, u32[]{:S(2)}) %collective-permute-start) | collective-permute-done | bytes 204832 | tf_op jit(solution)/shard_map/ppermute | solution.py:23
  17.7 1.5 collective-permute-start.1
  19.2 0.0 collective-permute-done.2
  19.2 4.6 %collective-permute-done.1 = bf16[80,1280]{1,0:T(8,128)(2,1)S(1)} collective-permute-done((bf16[80,1280]{1,0:T(8,128)(2,1)S(1)}, bf16[80,1280]{1,0:T(8,128)(2,1)S(1)}, u32[]{:S(2)}, u32[]{:S(2)}) %collective-permute-start.1) | collective-permute-done | bytes 204832 | tf_op jit(solution)/shard_map/ppermute | solution.py:23
  23.8 1.0 pad_maximum_fusion
  24.9 0.6 gather_fusion
  25.5 0.1 copy.10
  25.6 78.8 %all-gather.3.cloned.1.call-done = bf16[5120,1280]{1,0:T(8,128)(2,1)} async-done(((bf16[80,1280]{1,0:T(8,128)(2,1)}), bf16[5120,1280]{1,0:T(8,128)(2,1)}) %all-gather.3.cloned.1.call-update) | async-done | bytes 13107216 | tf_op jit(solution)/shard_map/all_gather | solution.py:62
  104.3 7.1 %fusion.23 = (bf16[80,1280]{1,0:T(8,128)(2,1)S(1)}, f32[80,1280]{1,0:T(8,128)S(1)}) fusion(f32[80,1280]{1,0:T(8,128)S(1)} %get-tuple-element.6, bf16[80,5120]{1,0:T(8,128)(2,1)S(1)} %bitcast.43, bf16[5120,1280]{1,0:T(8,128)(2,1)} %all-gather.3.cloned.1.call-done), kind=kOutput, calls=%fused_computation.52 | convolution fusion | flops 1048780800 | bytes 14950400 | tf_op jit(solution)/shard_map/dot_general | solution.py:65
  111.4 1.5 collective-permute-start.3
  113.0 0.6 collective-permute-start.5
  113.5 5.2 %collective-permute-done.3 = bf16[80,1280]{1,0:T(8,128)(2,1)S(1)} collective-permute-done((bf16[80,1280]{1,0:T(8,128)(2,1)S(1)}, bf16[80,1280]{1,0:T(8,128)(2,1)S(1)}, u32[]{:S(2)}, u32[]{:S(2)}) %collective-permute-start.3) | collective-permute-done | bytes 204832 | tf_op jit(solution)/shard_map/ppermute | solution.py:23
  118.7 1.5 collective-permute-start.4
  120.2 0.0 collective-permute-done.5
  120.2 4.9 %collective-permute-done.4 = bf16[80,1280]{1,0:T(8,128)(2,1)S(1)} collective-permute-done((bf16[80,1280]{1,0:T(8,128)(2,1)S(1)}, bf16[80,1280]{1,0:T(8,128)(2,1)S(1)}, u32[]{:S(2)}, u32[]{:S(2)}) %collective-permute-start.4) | collective-permute-done | bytes 204832 | tf_op jit(solution)/shard_map/ppermute | solution.py:23
  125.1 0.1 pad_maximum_fusion.1
  125.2 0.6 gather_fusion.1
  125.8 0.1 copy.11
  125.9 7.8 %fusion.4 = bf16[80,1280]{1,0:T(8,128)(2,1)} fusion(f32[80,1280]{1,0:T(8,128)S(1)} %get-tuple-element.6, bf16[80,5120]{1,0:T(8,128)(2,1)S(1)} %bitcast.46, bf16[5120,1280]{1,0:T(8,128)(2,1)} %all-gather.3.cloned.1.call-done, f32[80,1280]{1,0:T(8,128)S(1)} %get-tuple-element.8), kind=kOutput, calls=%fused_computation.12 | convolution fusion | flops 1049088000 | bytes 14950400 | tf_op jit(solution)/shard_map/dot_general | solution.py:65
  133.7 0.0 all-gather.5.cloned.1.call-update
  133.7 1.5 collective-permute-start.6
  135.2 1.6 collective-permute-start.8
  136.8 3.9 %collective-permute-done.6 = bf16[80,1280]{1,0:T(8,128)(2,1)S(1)} collective-permute-done((bf16[80,1280]{1,0:T(8,128)(2,1)}, bf16[80,1280]{1,0:T(8,128)(2,1)S(1)}, u32[]{:S(2)}, u32[]{:S(2)}) %collective-permute-start.6) | collective-permute-done | bytes 204832 | tf_op jit(solution)/shard_map/ppermute | solution.py:23
  140.7 0.5 collective-permute-start.7
  141.2 0.0 collective-permute-done.8
  141.2 6.5 %collective-permute-done.7 = bf16[80,1280]{1,0:T(8,128)(2,1)S(1)} collective-permute-done((bf16[80,1280]{1,0:T(8,128)(2,1)S(1)}, bf16[80,1280]{1,0:T(8,128)(2,1)S(1)}, u32[]{:S(2)}, u32[]{:S(2)}) %collective-permute-start.7) | collective-permute-done | bytes 204832 | tf_op jit(solution)/shard_map/ppermute | solution.py:23
  147.7 1.0 pad_maximum_fusion.2
  148.7 0.6 gather_fusion.2
  149.3 0.1 copy.12
  149.4 72.1 %all-gather.5.cloned.1.call-done = bf16[5120,1280]{1,0:T(8,128)(2,1)} async-done(((bf16[80,1280]{1,0:T(8,128)(2,1)}), bf16[5120,1280]{1,0:T(8,128)(2,1)}) %all-gather.5.cloned.1.call-update) | async-done | bytes 13107216 | tf_op jit(solution)/shard_map/all_gather | solution.py:62
  221.5 7.1 %fusion.24 = (bf16[80,1280]{1,0:T(8,128)(2,1)S(1)}, f32[80,1280]{1,0:T(8,128)S(1)}) fusion(f32[80,1280]{1,0:T(8,128)S(1)} %get-tuple-element.6, bf16[80,5120]{1,0:T(8,128)(2,1)S(1)} %bitcast.44, bf16[5120,1280]{1,0:T(8,128)(2,1)} %all-gather.5.cloned.1.call-done), kind=kOutput, calls=%fused_computation.53 | convolution fusion | flops 1048780800 | bytes 14950400 | tf_op jit(solution)/shard_map/dot_general | solution.py:65
  228.6 1.5 collective-permute-start.9
  230.1 0.6 collective-permute-start.11
  230.7 5.2 %collective-permute-done.9 = bf16[80,1280]{1,0:T(8,128)(2,1)S(1)} collective-permute-done((bf16[80,1280]{1,0:T(8,128)(2,1)S(1)}, bf16[80,1280]{1,0:T(8,128)(2,1)S(1)}, u32[]{:S(2)}, u32[]{:S(2)}) %collective-permute-start.9) | collective-permute-done | bytes 204832 | tf_op jit(solution)/shard_map/ppermute | solution.py:23
  235.9 1.5 collective-permute-start.10
  237.4 0.0 collective-permute-done.11
  237.4 4.9 %collective-permute-done.10 = bf16[80,1280]{1,0:T(8,128)(2,1)S(1)} collective-permute-done((bf16[80,1280]{1,0:T(8,128)(2,1)S(1)}, bf16[80,1280]{1,0:T(8,128)(2,1)S(1)}, u32[]{:S(2)}, u32[]{:S(2)}) %collective-permute-start.10) | collective-permute-done | bytes 204832 | tf_op jit(solution)/shard_map/ppermute | solution.py:23
  242.3 0.1 pad_maximum_fusion.3
  242.4 0.6 gather_fusion.3
  243.0 0.1 copy.13
  243.1 7.9 %fusion.2 = f32[80,1280]{1,0:T(8,128)} fusion(f32[80,1280]{1,0:T(8,128)S(1)} %get-tuple-element.6, bf16[80,5120]{1,0:T(8,128)(2,1)S(1)} %bitcast.45, bf16[5120,1280]{1,0:T(8,128)(2,1)} %all-gather.5.cloned.1.call-done, f32[80,1280]{1,0:T(8,128)S(1)} %get-tuple-element.10), kind=kOutput, calls=%fused_computation.10 | convolution fusion | flops 1048985600 | bytes 15155200 | tf_op jit(solution)/shard_map/dot_general | solution.py:65
  (4 shorter events, 0.0 us)
Async XLA Ops:
  6.5 97.8 %all-gather.3.cloned.1.call-start = ((), (), s32[]{:S(2)}) async-start(), calls=%async_computation | async-start | bytes 13312000 | tf_op jit(solution)/shard_map/all_gather | solution.py:62
  10.6 210.9 %all-gather.5.cloned.1.call-start = ((), (), s32[]{:S(2)}) async-start(), calls=%async_computation.1 | async-start | bytes 13312000 | tf_op jit(solution)/shard_map/all_gather | solution.py:62
  10.6 7.1 %collective-permute-start = (bf16[80,1280]{1,0:T(8,128)(2,1)}, bf16[80,1280]{1,0:T(8,128)(2,1)S(1)}, u32[]{:S(2)}, u32[]{:S(2)}) collective-permute-start(bf16[80,1280]{1,0:T(8,128)(2,1)} %get-tuple-element.5), channel_id=1, source_target_pairs={{0,8},{8,16},{16,24},{24,0},{1,9},{9,17},{17,25},{25,1},{2,10},{10... | collective-permute-start | bytes 614408 | tf_op jit(solution)/shard_map/ppermute | solution.py:23
  12.2 7.1 %collective-permute-start.2 = (bf16[80,1280]{1,0:T(8,128)(2,1)}, bf16[80,1280]{1,0:T(8,128)(2,1)S(1)}, u32[]{:S(2)}, u32[]{:S(2)}) collective-permute-start(bf16[80,1280]{1,0:T(8,128)(2,1)} %get-tuple-element.5), channel_id=1, source_target_pairs={{8,0},{16,8},{24,16},{0,24},{9,1},{17,9},{25,17},{1,25},{10,2},{18... | collective-permute-start | bytes 614408 | tf_op jit(solution)/shard_map/ppermute | solution.py:25
  17.7 6.1 %collective-permute-start.1 = (bf16[80,1280]{1,0:T(8,128)(2,1)S(1)}, bf16[80,1280]{1,0:T(8,128)(2,1)S(1)}, u32[]{:S(2)}, u32[]{:S(2)}) collective-permute-start(bf16[80,1280]{1,0:T(8,128)(2,1)S(1)} %collective-permute-done), channel_id=1, source_target_pairs={{0,8},{8,16},{16,24},{24,0},{1,9},{9,17},{17,25},{25,1},{2,10},{10... | collective-permute-start | bytes 614408 | tf_op jit(solution)/shard_map/ppermute | solution.py:23
  111.4 7.3 %collective-permute-start.3 = (bf16[80,1280]{1,0:T(8,128)(2,1)S(1)}, bf16[80,1280]{1,0:T(8,128)(2,1)S(1)}, u32[]{:S(2)}, u32[]{:S(2)}) collective-permute-start(bf16[80,1280]{1,0:T(8,128)(2,1)S(1)} %get-tuple-element.7), channel_id=1, source_target_pairs={{0,8},{8,16},{16,24},{24,0},{1,9},{9,17},{17,25},{25,1},{2,10},{10... | collective-permute-start | bytes 614408 | tf_op jit(solution)/shard_map/ppermute | solution.py:23
  113.0 7.2 %collective-permute-start.5 = (bf16[80,1280]{1,0:T(8,128)(2,1)S(1)}, bf16[80,1280]{1,0:T(8,128)(2,1)S(1)}, u32[]{:S(2)}, u32[]{:S(2)}) collective-permute-start(bf16[80,1280]{1,0:T(8,128)(2,1)S(1)} %get-tuple-element.7), channel_id=1, source_target_pairs={{8,0},{16,8},{24,16},{0,24},{9,1},{17,9},{25,17},{1,25},{10,2},{18... | collective-permute-start | bytes 614408 | tf_op jit(solution)/shard_map/ppermute | solution.py:25
  118.7 6.4 %collective-permute-start.4 = (bf16[80,1280]{1,0:T(8,128)(2,1)S(1)}, bf16[80,1280]{1,0:T(8,128)(2,1)S(1)}, u32[]{:S(2)}, u32[]{:S(2)}) collective-permute-start(bf16[80,1280]{1,0:T(8,128)(2,1)S(1)} %collective-permute-done.3), channel_id=1, source_target_pairs={{0,8},{8,16},{16,24},{24,0},{1,9},{9,17},{17,25},{25,1},{2,10},{10... | collective-permute-start | bytes 614408 | tf_op jit(solution)/shard_map/ppermute | solution.py:23
  133.7 7.0 %collective-permute-start.6 = (bf16[80,1280]{1,0:T(8,128)(2,1)}, bf16[80,1280]{1,0:T(8,128)(2,1)S(1)}, u32[]{:S(2)}, u32[]{:S(2)}) collective-permute-start(bf16[80,1280]{1,0:T(8,128)(2,1)} %fusion.4), channel_id=1, source_target_pairs={{0,8},{8,16},{16,24},{24,0},{1,9},{9,17},{17,25},{25,1},{2,10},{10... | collective-permute-start | bytes 614408 | tf_op jit(solution)/shard_map/ppermute | solution.py:23
  135.2 6.0 %collective-permute-start.8 = (bf16[80,1280]{1,0:T(8,128)(2,1)}, bf16[80,1280]{1,0:T(8,128)(2,1)S(1)}, u32[]{:S(2)}, u32[]{:S(2)}) collective-permute-start(bf16[80,1280]{1,0:T(8,128)(2,1)} %fusion.4), channel_id=1, source_target_pairs={{8,0},{16,8},{24,16},{0,24},{9,1},{17,9},{25,17},{1,25},{10,2},{18... | collective-permute-start | bytes 614408 | tf_op jit(solution)/shard_map/ppermute | solution.py:25
  140.7 6.9 %collective-permute-start.7 = (bf16[80,1280]{1,0:T(8,128)(2,1)S(1)}, bf16[80,1280]{1,0:T(8,128)(2,1)S(1)}, u32[]{:S(2)}, u32[]{:S(2)}) collective-permute-start(bf16[80,1280]{1,0:T(8,128)(2,1)S(1)} %collective-permute-done.6), channel_id=1, source_target_pairs={{0,8},{8,16},{16,24},{24,0},{1,9},{9,17},{17,25},{25,1},{2,10},{10... | collective-permute-start | bytes 614408 | tf_op jit(solution)/shard_map/ppermute | solution.py:23
  228.6 7.3 %collective-permute-start.9 = (bf16[80,1280]{1,0:T(8,128)(2,1)S(1)}, bf16[80,1280]{1,0:T(8,128)(2,1)S(1)}, u32[]{:S(2)}, u32[]{:S(2)}) collective-permute-start(bf16[80,1280]{1,0:T(8,128)(2,1)S(1)} %get-tuple-element.9), channel_id=1, source_target_pairs={{0,8},{8,16},{16,24},{24,0},{1,9},{9,17},{17,25},{25,1},{2,10},{10... | collective-permute-start | bytes 614408 | tf_op jit(solution)/shard_map/ppermute | solution.py:23
  230.1 7.2 %collective-permute-start.11 = (bf16[80,1280]{1,0:T(8,128)(2,1)S(1)}, bf16[80,1280]{1,0:T(8,128)(2,1)S(1)}, u32[]{:S(2)}, u32[]{:S(2)}) collective-permute-start(bf16[80,1280]{1,0:T(8,128)(2,1)S(1)} %get-tuple-element.9), channel_id=1, source_target_pairs={{8,0},{16,8},{24,16},{0,24},{9,1},{17,9},{25,17},{1,25},{10,2},{18... | collective-permute-start | bytes 614408 | tf_op jit(solution)/shard_map/ppermute | solution.py:25
  235.9 6.4 %collective-permute-start.10 = (bf16[80,1280]{1,0:T(8,128)(2,1)S(1)}, bf16[80,1280]{1,0:T(8,128)(2,1)S(1)}, u32[]{:S(2)}, u32[]{:S(2)}) collective-permute-start(bf16[80,1280]{1,0:T(8,128)(2,1)S(1)} %collective-permute-done.9), channel_id=1, source_target_pairs={{0,8},{8,16},{16,24},{24,0},{1,9},{9,17},{17,25},{25,1},{2,10},{10... | collective-permute-start | bytes 614408 | tf_op jit(solution)/shard_map/ppermute | solution.py:23
Sparse Core Ops, SparseCore 0:
  10.7 93.5 all-gather.2
  133.8 87.6 all-gather.4
